TPU v7x, 256 devices: a whole 4x4x8 slice. The times are simulated.
256 devices in a mesh: gx: 16 (over y_lo, z), gy: 16 (over y_hi, x, core).
Axes of the slice: x: 4, y: 4 (y_hi: 2, y_lo: 2; y = y_hi * 2 + y_lo), z: 8, core: 2. Of those that a mesh axis runs over, the one named last changes fastest.
Arguments:
- wide_index: int32 [4, 32, 2048], replicated, may hold values from 0 to 131071
- wide_table: bfloat16 [4, 131072, 256], P(None, ('gx', 'gy')), may hold values from -1.09375 to 1.09375
- wide_proj: bfloat16 [4, 256, 128], replicated, may hold values from -0.375 to 0.375
- thin_index: int32 [8, 32, 2048], P(None, None, 'gx'), may hold values from 0 to 65535
- thin_table: bfloat16 [8, 32, 65536], P(None, None, 'gy'), may hold values from -1.09375 to 1.09375
- thin_proj: bfloat16 [8, 32, 128], replicated, may hold values from -1 to 1
Outputs:
- wide_out: float32 [2048, 512], P(('gx', 'gy'))
- thin_out: float32 [2048, 1024], P(('gx', 'gy'))
All inputs are finite; a program needn't handle non-finite values.
Results may differ from a plain program's by a relative error of at most 0.0003.
Values sent between devices are 32-bit elements; how exact they have to be, the bound alone decides.
A program may use at most 64 MiB of HBM per device.

v0:
```python
import math

import jax
import jax.numpy as jnp
from jax import lax
from jax.sharding import Mesh
from jax.sharding import PartitionSpec as P

GX_GY = ("gx_0", "gx_1", "gy")
GX = ("gx_0", "gx_1")


def reduced_to_own(blocks, axes, turns):
    dims = [lax.axis_size(a) for a in axes]
    blocks = blocks.reshape(*dims, *blocks.shape[1:])
    blocks = blocks.transpose(*turns, *range(len(axes), blocks.ndim))
    blocks = blocks.reshape(-1, *blocks.shape[len(axes) :])
    for k in turns:
        blocks = lax.psum_scatter(blocks, axes[k], scatter_dimension=0, tiled=True)
    return blocks[0]


def split_up(shard, dim, count):
    before, after = (shard.shape[:dim], shard.shape[dim + 1 :])
    return jnp.moveaxis(shard.reshape(*before, count, -1, *after), dim, 0)


def sum_by_axis(shard, axes, turns, dim):
    count = lax.axis_size(axes)
    return reduced_to_own(split_up(shard, dim, count), axes, turns)


def summed_on_arrival(shard, axis, dim):
    count = lax.axis_size(axis)
    blocks = lax.all_to_all(split_up(shard, dim, count), axis, 0, 0, tiled=True)
    return jnp.sum(blocks, axis=0)


def blockwise(index_rows, compute):
    depth, amount = index_rows.shape
    block_size = math.gcd(amount, 512)
    grouped = index_rows.reshape(depth, amount // block_size, block_size).transpose(1, 0, 2)
    result = lax.map(compute, grouped)
    return result.reshape(amount, result.shape[-1])


def hit_counts(block_index, row_ids):
    return jnp.sum((block_index[:, :, None] == row_ids[None, None, :]).astype(jnp.bfloat16), axis=0)


def project(pooled, weight):
    return jnp.dot(pooled, weight.astype(jnp.float32), precision=lax.Precision.HIGHEST)


def wide_pool(wide_index, wide_table):
    row_count = wide_table.shape[1]
    row_ids = jnp.arange(row_count, dtype=jnp.int32)
    window = wide_index - lax.axis_index(GX_GY) * row_count
    pooled_list = []
    for which in range(wide_table.shape[0]):

        def compute(block_index, which=which):
            return jnp.dot(
                hit_counts(block_index, row_ids),
                wide_table[which],
                preferred_element_type=jnp.float32,
            )

        pooled_list.append(blockwise(window[which], compute))
    return pooled_list


def wide_project(pooled_list, wide_proj):
    return jnp.concatenate(
        [project(pooled, wide_proj[which]) for which, pooled in enumerate(pooled_list)], axis=1
    )


def thin_pool(thin_index, thin_table):
    row_count = thin_table.shape[2]
    row_ids = jnp.arange(row_count, dtype=jnp.int32)
    window = thin_index - lax.axis_index("gy") * row_count
    pooled_list = []
    for which in range(thin_table.shape[0]):

        def compute(block_index, which=which):
            return lax.dot_general(
                hit_counts(block_index, row_ids),
                thin_table[which],
                (((1,), (1,)), ((), ())),
                preferred_element_type=jnp.float32,
            )

        pooled_list.append(blockwise(window[which], compute))
    return pooled_list


def local(wide_index, wide_table, wide_proj, thin_index, thin_table, thin_proj):
    pooled_wide = wide_pool(wide_index, wide_table)
    partial_sum = wide_project(pooled_wide, wide_proj)
    across = sum_by_axis(partial_sum, GX, (1, 0), 0)
    wide_sums = summed_on_arrival(across, "gy", 0)
    pooled_thin = thin_pool(thin_index, thin_table)
    projected = jnp.concatenate(
        [project(pooled, thin_proj[which]) for which, pooled in enumerate(pooled_thin)], axis=1
    )
    thin_sums = summed_on_arrival(projected, "gy", 0)
    return (wide_sums, thin_sums)


def solution(mesh):
    finer = Mesh(mesh.devices.reshape(2, 8, mesh.shape["gy"]), ("gx_0", "gx_1", "gy"))
    placed = (P(), P(None, GX_GY, None), P(), P(None, None, GX), P(None, None, "gy"), P())
    return jax.shard_map(
        local,
        mesh=finer,
        in_specs=placed,
        out_specs=(P(GX_GY, None), P(GX_GY, None)),
        check_vma=False,
    )
```

profile of v0, /device:TPU:8, one launch (start us, length us, event | category | flops | bytes accessed | tf_op | source)
XLA Modules:
  0.0 254.2 jit_solution(12698831724754283663)
XLA Ops:
  9.9 17.8 %while.39 = (s32[]{:T(128)}, f32[4,512,256]{2,1,0:T(8,128)S(1)}, s32[4,32,512]{2,0,1:T(4,128)S(1)}, bf16[4,512,256]{2,1,0:T(8,128)(2,1)S(1)}, s32[]{:T(128)}) while((s32[]{:T(128)}, f32[4,512,256]{2,1,0:T(8,128)S(1)}, s32[4,32,512]{2,0,1:T(4,128)S(1)}, bf16[4,512,256]{2,1,0:T(8,128)(2,1)S(1)}, s32[]{:T(128)}) %tuple.164), condition=%wide.region_11.12_spmd.clone, body=%wide.region_9.11_spmd.clone.sunk | while | flops 159121408 | bytes 2162765 | solution.py:43
  10.0 4.0 %fusion.151 = bf16[512,512]{1,0:T(8,128)(2,1)S(1)} fusion(s32[32,512]{1,0:T(8,128)S(1)} %bitcast.197), kind=kLoop, calls=%fused_computation.33.clone.1 | loop fusion | flops 24903680 | bytes 589824 | tf_op jit(solution)/shard_map/while/body/eval_jaxpr/reduce_sum | solution.py:48
  14.4 4.0 %fusion.151 = bf16[512,512]{1,0:T(8,128)(2,1)S(1)} fusion(s32[32,512]{1,0:T(8,128)S(1)} %bitcast.197), kind=kLoop, calls=%fused_computation.33.clone.1 | loop fusion | flops 24903680 | bytes 589824 | tf_op jit(solution)/shard_map/while/body/eval_jaxpr/reduce_sum | solution.py:48
  18.9 4.0 %fusion.151 = bf16[512,512]{1,0:T(8,128)(2,1)S(1)} fusion(s32[32,512]{1,0:T(8,128)S(1)} %bitcast.197), kind=kLoop, calls=%fused_computation.33.clone.1 | loop fusion | flops 24903680 | bytes 589824 | tf_op jit(solution)/shard_map/while/body/eval_jaxpr/reduce_sum | solution.py:48
  23.3 4.0 %fusion.151 = bf16[512,512]{1,0:T(8,128)(2,1)S(1)} fusion(s32[32,512]{1,0:T(8,128)S(1)} %bitcast.197), kind=kLoop, calls=%fused_computation.33.clone.1 | loop fusion | flops 24903680 | bytes 589824 | tf_op jit(solution)/shard_map/while/body/eval_jaxpr/reduce_sum | solution.py:48
  30.4 21.0 %while.38 = (s32[]{:T(128)}, f32[4,512,256]{2,1,0:T(8,128)}, s32[4,32,512]{2,0,1:T(4,128)S(1)}, bf16[4,512,256]{2,1,0:T(8,128)(2,1)S(1)}, s32[]{:T(128)}) while((s32[]{:T(128)}, f32[4,512,256]{2,1,0:T(8,128)}, s32[4,32,512]{2,0,1:T(4,128)S(1)}, bf16[4,512,256]{2,1,0:T(8,128)(2,1)S(1)}, s32[]{:T(128)}) %tuple.165), condition=%wide.region_8.9_spmd.clone, body=%wide.region_6.8_spmd.clone.sunk | while | flops 159121408 | bytes 2162765 | solution.py:43
  30.5 4.0 %fusion.147 = bf16[512,512]{1,0:T(8,128)(2,1)S(1)} fusion(s32[32,512]{1,0:T(8,128)S(1)} %bitcast.198), kind=kLoop, calls=%fused_computation.24.clone.1 | loop fusion | flops 24903680 | bytes 589824 | tf_op jit(solution)/shard_map/while/body/eval_jaxpr/reduce_sum | solution.py:48
  35.7 4.0 %fusion.147 = bf16[512,512]{1,0:T(8,128)(2,1)S(1)} fusion(s32[32,512]{1,0:T(8,128)S(1)} %bitcast.198), kind=kLoop, calls=%fused_computation.24.clone.1 | loop fusion | flops 24903680 | bytes 589824 | tf_op jit(solution)/shard_map/while/body/eval_jaxpr/reduce_sum | solution.py:48
  40.9 4.0 %fusion.147 = bf16[512,512]{1,0:T(8,128)(2,1)S(1)} fusion(s32[32,512]{1,0:T(8,128)S(1)} %bitcast.198), kind=kLoop, calls=%fused_computation.24.clone.1 | loop fusion | flops 24903680 | bytes 589824 | tf_op jit(solution)/shard_map/while/body/eval_jaxpr/reduce_sum | solution.py:48
  46.2 4.0 %fusion.147 = bf16[512,512]{1,0:T(8,128)(2,1)S(1)} fusion(s32[32,512]{1,0:T(8,128)S(1)} %bitcast.198), kind=kLoop, calls=%fused_computation.24.clone.1 | loop fusion | flops 24903680 | bytes 589824 | tf_op jit(solution)/shard_map/while/body/eval_jaxpr/reduce_sum | solution.py:48
  59.0 17.8 %while.37 = (s32[]{:T(128)}, f32[4,512,256]{2,1,0:T(8,128)S(1)}, s32[4,32,512]{2,0,1:T(4,128)S(1)}, bf16[4,512,256]{2,1,0:T(8,128)(2,1)S(1)}, s32[]{:T(128)}) while((s32[]{:T(128)}, f32[4,512,256]{2,1,0:T(8,128)S(1)}, s32[4,32,512]{2,0,1:T(4,128)S(1)}, bf16[4,512,256]{2,1,0:T(8,128)(2,1)S(1)}, s32[]{:T(128)}) %tuple.166), condition=%wide.region_5.6_spmd.clone, body=%wide.region_3.5_spmd.clone.sunk | while | flops 159121408 | bytes 2162765 | solution.py:43
  59.1 4.0 %fusion.143 = bf16[512,512]{1,0:T(8,128)(2,1)S(1)} fusion(s32[32,512]{1,0:T(8,128)S(1)} %bitcast.199), kind=kLoop, calls=%fused_computation.15.clone.1 | loop fusion | flops 24903680 | bytes 589824 | tf_op jit(solution)/shard_map/while/body/eval_jaxpr/reduce_sum | solution.py:48
  63.6 4.0 %fusion.143 = bf16[512,512]{1,0:T(8,128)(2,1)S(1)} fusion(s32[32,512]{1,0:T(8,128)S(1)} %bitcast.199), kind=kLoop, calls=%fused_computation.15.clone.1 | loop fusion | flops 24903680 | bytes 589824 | tf_op jit(solution)/shard_map/while/body/eval_jaxpr/reduce_sum | solution.py:48
  72.5 4.0 %fusion.143 = bf16[512,512]{1,0:T(8,128)(2,1)S(1)} fusion(s32[32,512]{1,0:T(8,128)S(1)} %bitcast.199), kind=kLoop, calls=%fused_computation.15.clone.1 | loop fusion | flops 24903680 | bytes 589824 | tf_op jit(solution)/shard_map/while/body/eval_jaxpr/reduce_sum | solution.py:48
  81.3 17.8 %while.36 = (s32[]{:T(128)}, f32[4,512,256]{2,1,0:T(8,128)S(1)}, s32[4,32,512]{2,0,1:T(4,128)S(1)}, bf16[4,512,256]{2,1,0:T(8,128)(2,1)S(1)}, s32[]{:T(128)}) while((s32[]{:T(128)}, f32[4,512,256]{2,1,0:T(8,128)S(1)}, s32[4,32,512]{2,0,1:T(4,128)S(1)}, bf16[4,512,256]{2,1,0:T(8,128)(2,1)S(1)}, s32[]{:T(128)}) %tuple.163), condition=%wide.region_2.3_spmd.clone, body=%wide.region_0.2_spmd.clone.sunk | while | flops 159121408 | bytes 2162765 | solution.py:43
  85.9 4.0 %fusion.139 = bf16[512,512]{1,0:T(8,128)(2,1)S(1)} fusion(s32[32,512]{1,0:T(8,128)S(1)} %bitcast.200), kind=kLoop, calls=%fused_computation.6.clone.1 | loop fusion | flops 24903680 | bytes 589824 | tf_op jit(solution)/shard_map/while/body/eval_jaxpr/reduce_sum | solution.py:48
  106.6 5.3 %copy.18 = f32[2,8,128,512]{3,2,0,1:T(8,128)} copy(f32[2,8,128,512]{2,1,0,3:T(8,128)} %bitcast.192) | data formatting | bytes 8388608 | tf_op jit(solution)/shard_map/reshape;reshape | solution.py:15
  112.8 20.9 %fusion.42 = (bf16[128,4096]{1,0:T(8,128)(2,1)S(1)}, bf16[128,4096]{1,0:T(8,128)(2,1)S(1)}) fusion(s32[32,128]{1,0:T(8,128)S(1)} %get-tuple-element.500, s32[32,128]{1,0:T(8,128)S(1)} %get-tuple-element.501), kind=kLoop, calls=%fused_computation.62 | loop fusion | flops 99614720 | bytes 2129920 | tf_op jit(solution)/shard_map/while/body/eval_jaxpr/reduce_sum | solution.py:48
  137.0 20.9 %fusion.40 = (bf16[128,4096]{1,0:T(8,128)(2,1)S(1)}, bf16[128,4096]{1,0:T(8,128)(2,1)S(1)}) fusion(s32[32,128]{1,0:T(8,128)S(1)} %get-tuple-element.498, s32[32,128]{1,0:T(8,128)S(1)} %get-tuple-element.499), kind=kLoop, calls=%fused_computation.60 | loop fusion | flops 99614720 | bytes 2129920 | tf_op jit(solution)/shard_map/while/body/eval_jaxpr/reduce_sum | solution.py:48
  161.3 20.9 %fusion.38 = (bf16[128,4096]{1,0:T(8,128)(2,1)S(1)}, bf16[128,4096]{1,0:T(8,128)(2,1)S(1)}) fusion(s32[32,128]{1,0:T(8,128)S(1)} %get-tuple-element.496, s32[32,128]{1,0:T(8,128)S(1)} %get-tuple-element.497), kind=kLoop, calls=%fused_computation.58 | loop fusion | flops 99614720 | bytes 2129920 | tf_op jit(solution)/shard_map/while/body/eval_jaxpr/reduce_sum | solution.py:48
  185.5 20.9 %fusion.36 = (bf16[128,4096]{1,0:T(8,128)(2,1)S(1)}, bf16[128,4096]{1,0:T(8,128)(2,1)S(1)}) fusion(s32[32,128]{1,0:T(8,128)S(1)} %get-tuple-element.494, s32[32,128]{1,0:T(8,128)S(1)} %get-tuple-element.495), kind=kLoop, calls=%fused_computation.56 | loop fusion | flops 99614720 | bytes 2129920 | tf_op jit(solution)/shard_map/while/body/eval_jaxpr/reduce_sum | solution.py:48
  210.0 18.3 %all_to_all.10 = f32[16,8,1024]{2,1,0:T(8,128)S(1)} all-to-all(f32[16,8,1024]{2,1,0:T(8,128)S(1)} %bitcast.201), channel_id=1, replica_groups=mesh['gx_0'=2,'gx_1'=8,'gy'=16] {'gy'}, dimensions={0} | all-to-all | bytes 1048576 | tf_op jit(solution)/shard_map/all_to_all | solution.py:35
  232.0 5.3 %all-to-all-start = ((f32[16,8,512]{2,1,0:T(8,128)}), f32[16,8,512]{2,1,0:T(8,128)S(1)}, u32[]{:S(2)}, u32[]{:S(2)}) async-start(f32[16,8,512]{2,1,0:T(8,128)} %bitcast.206), calls=%async_computation.2 | async-start | bytes 524288 | tf_op jit(solution)/shard_map/all_to_all | solution.py:35
  238.0 8.7 %all-to-all-done = f32[16,8,512]{2,1,0:T(8,128)S(1)} async-done(((f32[16,8,512]{2,1,0:T(8,128)}), f32[16,8,512]{2,1,0:T(8,128)S(1)}, u32[]{:S(2)}, u32[]{:S(2)}) %all-to-all-start) | async-done | bytes 262176 | tf_op jit(solution)/shard_map/all_to_all | solution.py:35
  (103 shorter events, 69.6 us)
Async XLA Ops:
  7.2 2.7 %copy-start = (bf16[4,512,256]{2,1,0:T(8,128)(2,1)S(1)}, bf16[4,512,256]{2,1,0:T(8,128)(2,1)}, u32[]{:S(2)}) copy-start(bf16[4,512,256]{2,1,0:T(8,128)(2,1)} %param.15) | copy-start | bytes 3145732
  7.2 200.6 %reduce-scatter.3.cloned.1.call-start = ((), (), s32[]{:S(2)}) async-start(), calls=%async_computation.4 | async-start | bytes 4718592 | tf_op jit(solution)/shard_map/reduce_scatter | solution.py:19
  51.3 3.3 %copy-start.1 = (f32[4,512,256]{2,1,0:T(8,128)S(1)}, f32[4,512,256]{2,1,0:T(8,128)}, u32[]{:S(2)}) copy-start(f32[4,512,256]{2,1,0:T(8,128)} %get-tuple-element.384) | copy-start | bytes 6291460
  111.9 0.9 copy-start.2
  111.9 23.3 %copy-start.3 = (bf16[8,32,128]{2,1,0:T(8,128)(2,1)S(1)}, bf16[8,32,128]{2,1,0:T(8,128)(2,1)}, u32[]{:S(2)}) copy-start(bf16[8,32,128]{2,1,0:T(8,128)(2,1)} %param.19) | copy-start | bytes 196612
  111.9 120.1 %reduce-scatter.5.cloned.1.call-start = ((), (), s32[]{:S(2)}) async-start(), calls=%async_computation.5 | async-start | bytes 786432 | tf_op jit(solution)/shard_map/reduce_scatter | solution.py:19
  232.0 14.7 %all-to-all-start = ((f32[16,8,512]{2,1,0:T(8,128)}), f32[16,8,512]{2,1,0:T(8,128)S(1)}, u32[]{:S(2)}, u32[]{:S(2)}) async-start(f32[16,8,512]{2,1,0:T(8,128)} %bitcast.206), calls=%async_computation.2 | async-start | bytes 524288 | tf_op jit(solution)/shard_map/all_to_all | solution.py:35
Sparse Core Ops, SparseCore 0:
  112.0 58.1 reduce-scatter.2
  208.0 24.0 reduce-scatter.4
where the time goes:
time: 257 us; the launch traced here: 254 us
  other arithmetic  153 us (60%)
  matrix products  33 us (13%)
  blocking collectives  18.3 us (7%)
  local copies, waits for them, and re-layouts  16.6 us (6%)
  between operations  14.3 us (6%)
  waiting for transfers between devices  12.6 us (5%)
  starting transfers between devices  5.57 us (2%)
    reduce_sum x20, other arithmetic, hit_counts(): jnp.sum((block_index[:, :, None] == row_ids[None, None, :]).astype(jnp.bf...  148 us
    all_to_all x1, blocking collectives, summed_on_arrival(): blocks = lax.all_to_all(split_up(shard, dim, count), axis, 0, 0, tiled=True)  18.3 us
    dot_general x12, matrix products, project(): jnp.dot(pooled, weight.astype(jnp.float32), precision=lax.Precision.HIGHEST)  13.8 us
    dot_general x8, matrix products, compute(): lax.dot_general(hit_counts(block_index, row_ids), thin_table[which], (((1...  11.2 us
    all_to_all x1, waiting for transfers between devices, summed_on_arrival(): blocks = lax.all_to_all(split_up(shard, dim, count), axis, 0, 0, tiled=True)  8.7 us
    dot_general x16, matrix products, compute(): jnp.dot(hit_counts(block_index, row_ids), wide_table[which], preferred_el...  8.02 us
    all_to_all x1, starting transfers between devices, summed_on_arrival(): blocks = lax.all_to_all(split_up(shard, dim, count), axis, 0, 0, tiled=True)  5.31 us
    another operation x1, local copies, waits for them, and re-layouts, reduced_to_own(): blocks = blocks.reshape(*dims, *blocks.shape[1:])  5.31 us
  transfers between devices with their start and end apart: 3, of which 2 were waited for; matrix products, arithmetic and copies ran while one was open for 38% of the time, Pallas kernels for 0%

commit v1 on v0

v1 whole, which is shorter than its diff:
```python
import jax
import jax.numpy as jnp
from jax import lax
from jax.experimental import pallas as pl
from jax.experimental.pallas import tpu as pltpu
from jax.sharding import PartitionSpec as P

F32, BF16, I32 = jnp.float32, jnp.bfloat16, jnp.int32
MESH = pl.DeviceIdType.MESH
GX_GY = ("gx", "gy")

WIDE_SLOTS = 2
THIN_SLOTS = 8
BLOCK = 256


def keys_of(index, first, count):
    row = index - first
    place = lax.broadcasted_iota(I32, row.shape, 0)
    return jnp.where((row >= 0) & (row < count), row * 32 + place, -1)


def next_slot(keys, slot):
    return jnp.max(jnp.where(keys < slot, keys, -1), axis=0, keepdims=True)


def tiled_row(values, rows):
    return jnp.broadcast_to(values, (rows, values.shape[1]))


def pool_kernel(wi, wt, wp, ti, tt, wide, thin, ids, keys, hits, proj, lines, low, sums):
    t = pl.program_id(0)
    gx, gy = lax.axis_index("gx"), lax.axis_index("gy")
    me = gx * 16 + gy
    rows_w = wt.shape[1]
    one, zero = jnp.ones((16, 128), BF16), jnp.zeros((16, 128), BF16)

    @pl.when(t == 0)
    def _():
        ids[...] = (lax.broadcasted_iota(I32, ids.shape, 0) - 256).astype(F32).astype(BF16)

    projected = jnp.dot(wt[0], wp[0], preferred_element_type=F32).T
    high = projected.astype(BF16)
    proj[:128] = high
    proj[128:] = (projected - high.astype(F32)).astype(BF16)

    all_keys = keys_of(wi[0], me * rows_w, rows_w)
    keys[...] = all_keys
    slots = [jnp.max(all_keys, axis=0, keepdims=True)]
    for _ in range(WIDE_SLOTS):
        slots.append(next_slot(all_keys, slots[-1]))

    def wide_id(slot):
        return tiled_row(jnp.where(slot < 0, 256, (slot >> 5) - 256).astype(F32), 16).astype(BF16)

    blocks = all_keys.shape[1] // BLOCK
    more = [jnp.max(slots[WIDE_SLOTS][:, b * BLOCK : (b + 1) * BLOCK]) for b in range(blocks)]
    for b in range(blocks):
        for c in range(BLOCK // 128):
            at = b * BLOCK + c * 128
            marks = [wide_id(s[:, at : at + 128]) for s in slots[:WIDE_SLOTS]]
            for r in range(rows_w // 16):
                here = ids[r * 16 : r * 16 + 16, :]
                hit = jnp.where(here == marks[0], one, zero)
                for mark in marks[1:]:
                    hit = hit + jnp.where(here == mark, one, zero)
                hits[r * 16 : r * 16 + 16, at : at + 128] = hit
    for b in range(blocks):

        @pl.when(more[b] >= 0)
        def _(b=b):
            block = slice(b * BLOCK, (b + 1) * BLOCK)

            def body(carry):
                slot, _ = carry
                for c in range(BLOCK // 128):
                    at = b * BLOCK + c * 128
                    mark = wide_id(slot[:, c * 128 : c * 128 + 128])
                    for r in range(rows_w // 16):
                        here = ids[r * 16 : r * 16 + 16, :]
                        spot = (slice(r * 16, r * 16 + 16), slice(at, at + 128))
                        hits[spot] = hits[spot] + jnp.where(here == mark, one, zero)
                slot = next_slot(keys[:, block], slot)
                return slot, jnp.max(slot)

            lax.while_loop(lambda carry: carry[1] >= 0, body, (slots[WIDE_SLOTS][:, block], more[b]))

    step = [(8 >> ((d - t + 4) % 4)) * 8 for d in range(4)]
    for b in range(blocks):
        both = jnp.dot(proj[...], hits[:, b * BLOCK : (b + 1) * BLOCK], preferred_element_type=F32)
        found = (both[:128] + both[128:]).T
        for g in range(BLOCK // 128):
            y_lo, z = divmod(b * (BLOCK // 128) + g, 8)
            for y_hi in range(2):
                for x in range(4):
                    bits = ((x // 2) ^ (x % 2), y_hi ^ y_lo, x // 2, y_hi)
                    place = sum((s for s, bit in zip(step, bits) if bit), z)
                    for core in range(2):
                        at = g * 128 + y_hi * 64 + x * 16 + core * 8
                        wide[0, core * 128 + place] = found[at : at + 8]

    rows_t = tt.shape[2]
    groups = rows_t // 256
    last = []
    for i in range(2):
        for g in range(groups):
            lines[i, g * 32 : g * 32 + 32, :] = tt[i, :, g * 256 : g * 256 + 256]
        thin_keys = keys_of(ti[i], gy * rows_t, rows_t)
        slot = jnp.max(thin_keys, axis=0, keepdims=True)
        taken = [slot]
        for _ in range(THIN_SLOTS):
            taken.append(next_slot(thin_keys, taken[-1]))
        last.append((thin_keys, taken[-1], jnp.max(taken[-1])))

        def mark_low(slot, at):
            mark = tiled_row(((slot >> 5) & 255).astype(F32), 16).astype(BF16)
            for r in range(16):
                here = ids[256 + r * 16 : 272 + r * 16, :]
                low[i, r * 16 : r * 16 + 16, at : at + 128] = jnp.where(here == mark, one, zero)

        def select(slot, found, total):
            group = tiled_row(slot >> 13, 8)
            picked = [jnp.zeros((8, 128), F32)] * 4
            for g in range(groups):
                same = group == g
                picked = [
                    jnp.where(same, found[g * 32 + f * 8 : g * 32 + f * 8 + 8], picked[f])
                    for f in range(4)
                ]
            return [a + b for a, b in zip(total, picked)]

        for k in range(THIN_SLOTS):
            mark_low(taken[k], k * 128)
        total = [jnp.zeros((8, 128), F32)] * 4
        for pair in range(THIN_SLOTS // 2):
            found = jnp.dot(
                lines[i], low[i, :, pair * 256 : pair * 256 + 256], preferred_element_type=F32
            )
            for k in range(2):
                total = select(taken[pair * 2 + k], found[:, k * 128 : k * 128 + 128], total)
        base = (t % 2) * 64 + i * 32
        for f in range(4):
            sums[pl.ds(pl.multiple_of(base + f * 8, 8), 8), :] = total[f]

    for i in range(2):
        thin_keys, slot, top = last[i]

        @pl.when(top >= 0)
        def _(i=i, slot=slot, top=top):
            base = (t % 2) * 64 + i * 32
            again = keys_of(ti[i], gy * rows_t, rows_t)

            def body(carry):
                slot, _ = carry
                mark = tiled_row(((slot >> 5) & 255).astype(F32), 16).astype(BF16)
                for r in range(16):
                    here = ids[256 + r * 16 : 272 + r * 16, :]
                    low[i, r * 16 : r * 16 + 16, :128] = jnp.where(here == mark, one, zero)
                found = jnp.dot(lines[i], low[i, :, :128], preferred_element_type=F32)
                group = tiled_row(slot >> 13, 8)
                for f in range(4):
                    spot = pl.ds(pl.multiple_of(base + f * 8, 8), 8)
                    total = sums[spot, :]
                    for g in range(groups):
                        piece = found[g * 32 + f * 8 : g * 32 + f * 8 + 8]
                        total = total + jnp.where(group == g, piece, 0.0)
                    sums[spot, :] = total
                slot = next_slot(again, slot)
                return slot, jnp.max(slot)

            lax.while_loop(lambda carry: carry[1] >= 0, body, (slot, top))

    @pl.when(t % 2 == 1)
    def _():
        thin[0] = sums[...].T


def pool(wide_index, wide_table, wide_proj, thin_index, thin_table):
    tw, depth, bags = wide_index.shape
    rows_w, ww = wide_table.shape[1:]
    per_step = thin_index.shape[0] // tw
    own_bags = thin_index.shape[2]
    wt, rows_t = thin_table.shape[1:]

    def block(shape):
        return pl.BlockSpec(shape, lambda t: (t, 0, 0))

    return pl.pallas_call(
        pool_kernel,
        grid=(tw,),
        in_specs=[
            block((1, depth, bags)),
            block((1, rows_w, ww)),
            block((1, ww, 128)),
            block((per_step, depth, own_bags)),
            block((per_step, wt, rows_t)),
        ],
        out_specs=[
            pl.BlockSpec((1, bags // 8, 8, 128), lambda t: (t, 0, 0, 0)),
            pl.BlockSpec((1, 128, 128), lambda t: (t // 2, 0, 0)),
        ],
        out_shape=[
            jax.ShapeDtypeStruct((tw, bags // 8, 8, 128), F32),
            jax.ShapeDtypeStruct((2, 128, 128), F32),
        ],
        scratch_shapes=[
            pltpu.VMEM((rows_w, 128), BF16),
            pltpu.VMEM((depth, bags), I32),
            pltpu.VMEM((rows_w, bags), BF16),
            pltpu.VMEM((256, rows_w), BF16),
            pltpu.VMEM((2, rows_t // 256 * wt, 256), BF16),
            pltpu.VMEM((2, 256, THIN_SLOTS * 128), BF16),
            pltpu.VMEM((128, 128), F32),
        ],
        compiler_params=pltpu.CompilerParams(dimension_semantics=("arbitrary",)),
    )(wide_index, wide_table, wide_proj, thin_index, thin_table)


def exchange_kernel(
    w, th, pj, wide_out, thin_out, own, r0, r1, r2, r3, r4, rz, rt,
    load, ssem, rsem, zs, zr, ts, tr,
):
    gx, gy = lax.axis_index("gx"), lax.axis_index("gy")
    y_lo, z = gx // 8, gx % 8
    y_hi, x, core = gy // 8, (gy // 2) % 4, gy % 2

    def gy_of(y_hi, x, core):
        return y_hi * 8 + x * 2 + core

    links = [
        ((gx, gy_of(y_hi, x + 1 - 2 * (x % 2), core)), (x // 2 + x % 2) % 2),
        (((1 - y_lo) * 8 + z, gy), (y_hi + y_lo) % 2),
        ((gx, gy_of(y_hi, 3 - x, core)), x // 2),
        (((1 - y_lo) * 8 + z, gy_of(1 - y_hi, x, core)), y_hi),
    ]
    other = (gx, gy_of(y_hi, x, 1 - core))
    along_z = [None] + [(y_lo * 8 + (z + d) % 8, gy) for d in range(1, 8)]
    along_gy = [None] + [(gx, (gy + d) % 16) for d in range(1, 16)]

    barrier = pltpu.get_barrier_semaphore()
    peers = along_gy[1:] + along_z[1:] + [links[1][0], links[3][0]]
    for peer in peers:
        pl.semaphore_signal(barrier, inc=1, device_id=peer, device_id_type=MESH)
    loads = []
    for c in range(4):
        loads.append(pltpu.make_async_copy(w.at[c, core], own.at[c], load.at[c]))
        loads[-1].start()
    pl.semaphore_wait(barrier, len(peers))

    def send(src, dst, s, r, to):
        copy = pltpu.make_async_remote_copy(
            src_ref=src, dst_ref=dst, send_sem=s, recv_sem=r, device_id=to, device_id_type=MESH
        )
        copy.start()
        return copy

    sends = []
    halves = []
    for c in range(4):
        halves.append(send(w.at[c, 1 - core], r0.at[c], ssem.at[0, c], rsem.at[0, c], other))
    thins = []
    for d in range(1, 16):
        thins.append(send(th.at[:, along_gy[d][1]], rt.at[d], ts.at[d], tr.at[d], along_gy[d]))

    held, got = [own.at[c] for c in range(4)], halves
    landed = [r0, r1, r2, r3, r4]
    bits = [[links[(c + k) % 4][1] for k in range(4)] for c in range(4)]
    partners = [[links[(c + k) % 4][0] for k in range(4)] for c in range(4)]

    def thin_part():
        for copy in thins:
            copy.wait_recv()
        pooled = th[:, gy]
        for d in range(1, 16):
            pooled = pooled + rt[d]
        group = lax.broadcasted_iota(I32, (8, 128), 1) // 32
        for h in range(2):
            parts = [jnp.where(group == g, pooled[h], 0.0) for g in range(4)]
            out = jnp.dot(
                jnp.concatenate(parts, axis=0),
                pj[h].astype(F32),
                preferred_element_type=F32,
                precision=lax.Precision.HIGHEST,
            )
            for g in range(4):
                at = (h * 4 + g) * 128
                thin_out[:, at : at + 128] = out[g * 8 : g * 8 + 8]

    for k in range(5):
        nxt = []
        for c in range(4):
            got[c].wait_recv()
            sends.append(got[c])
            new = landed[k]
            if k == 0:
                loads[c].wait()
            kept = bits[c][k - 1] if k > 0 else None
            if k < 4:
                go, stay = 1 - bits[c][k], bits[c][k]
                for part in (go, stay):
                    if k == 0:
                        own[c, part] = own[c, part] + r0[c, part]
                    elif k == 1:
                        new[c, part] = new[c, part] + own[c, kept, part]
                    else:
                        new[c, part] = new[c, part] + landed[k - 1][c, kept, part]
                    if part is go:
                        source = own if k == 0 else new
                        nxt.append(
                            send(
                                source.at[c, go],
                                landed[k + 1].at[c],
                                ssem.at[k + 1, c],
                                rsem.at[k + 1, c],
                                partners[c][k],
                            )
                        )
            else:
                new[c] = new[c] + landed[k - 1][c, kept]
        got = nxt
        if k == 0:
            thin_part()

    lasts = []
    for d in range(1, 8):
        lasts.append(
            send(r4.at[:, (z + d) % 8], rz.at[d], zs.at[d], zr.at[d], along_z[d])
        )
    total = r4[:, z]
    for d in range(1, 8):
        lasts[d - 1].wait_recv()
        total = total + rz[d]
    for c in range(4):
        wide_out[:, c * 128 : c * 128 + 128] = total[c]
    for copy in sends + lasts + thins:
        copy.wait_send()


def exchange(wide, thin, thin_proj):
    wide = wide.reshape(4, 2, 2, 2, 2, 2, 8, 8, 128)
    thin = thin.reshape(2, 16, 8, 128)
    proj = thin_proj.reshape(2, 128, 128)
    vmem = pl.BlockSpec(memory_space=pltpu.VMEM)
    dma = pltpu.SemaphoreType.DMA
    return pl.pallas_call(
        exchange_kernel,
        in_specs=[pl.BlockSpec(memory_space=pl.ANY), vmem, vmem],
        out_specs=[vmem, vmem],
        out_shape=[
            jax.ShapeDtypeStruct((8, 512), F32),
            jax.ShapeDtypeStruct((8, 1024), F32),
        ],
        scratch_shapes=[
            pltpu.VMEM((4, 2, 2, 2, 2, 8, 8, 128), F32),
            pltpu.VMEM((4, 2, 2, 2, 2, 8, 8, 128), F32),
            pltpu.VMEM((4, 2, 2, 2, 8, 8, 128), F32),
            pltpu.VMEM((4, 2, 2, 8, 8, 128), F32),
            pltpu.VMEM((4, 2, 8, 8, 128), F32),
            pltpu.VMEM((4, 8, 8, 128), F32),
            pltpu.VMEM((8, 4, 8, 128), F32),
            pltpu.VMEM((16, 2, 8, 128), F32),
            dma((4,)),
            dma((5, 4)),
            dma((5, 4)),
            dma((8,)),
            dma((8,)),
            dma((16,)),
            dma((16,)),
        ],
        compiler_params=pltpu.CompilerParams(collective_id=0, has_side_effects=True),
    )(wide, thin, proj)


def local(wide_index, wide_table, wide_proj, thin_index, thin_table, thin_proj):
    wide, thin = pool(wide_index, wide_table, wide_proj, thin_index, thin_table)
    return exchange(wide, thin, thin_proj)


def solution(mesh):
    placed = (P(), P(None, GX_GY, None), P(), P(None, None, "gx"), P(None, None, "gy"), P())
    return jax.shard_map(
        local,
        mesh=mesh,
        in_specs=placed,
        out_specs=(P(GX_GY, None), P(GX_GY, None)),
        check_vma=False,
    )
```

time: 257 us -> 60.6 us (0.24)
  other arithmetic: 153 us -> 0 us
  Pallas kernels: 0 us -> 56.8 us
  matrix products: 33 us -> 0 us
  blocking collectives: 18.3 us -> 0 us
  local copies, waits for them, and re-layouts: 16.6 us -> 2.7 us
  between operations: 14.3 us -> 0.64 us
  waiting for transfers between devices: 12.6 us -> 0 us
  starting transfers between devices: 5.57 us -> 0 us
    reduce_sum x22 -> x0, other arithmetic: 150 us -> none  [the longest x20 148 us: hit_counts(): jnp.sum((block_index[:, :, None] == row_ids[None, None, :]).astype(jnp.bf...]
    pallas_call x0 -> x2, Pallas kernels: none -> 56.8 us  [the longest x1 40.4 us: exchange(): pl.pallas_call(exchange_kernel, in_specs=[pl.BlockSpec(memory_space=pl.AN...]
    dot_general x36 -> x0, matrix products: 33 us -> none  [the longest x12 13.8 us: project(): jnp.dot(pooled, weight.astype(jnp.float32), precision=lax.Precision.HIGHEST)]
    all_to_all x1 -> x0, blocking collectives: 18.3 us -> none  [summed_on_arrival(): blocks = lax.all_to_all(split_up(shard, dim, count), axis, 0, 0, tiled=True)]
    another operation x9 -> x0, local copies, waits for them, and re-layouts: 10.9 us -> none  [the longest x1 5.31 us: reduced_to_own(): blocks = blocks.reshape(*dims, *blocks.shape[1:])]
    all_to_all x1 -> x0, waiting for transfers between devices: 8.7 us -> none  [summed_on_arrival(): blocks = lax.all_to_all(split_up(shard, dim, count), axis, 0, 0, tiled=True)]
    all_to_all x1 -> x0, starting transfers between devices: 5.31 us -> none  [summed_on_arrival(): blocks = lax.all_to_all(split_up(shard, dim, count), axis, 0, 0, tiled=True)]
    reduce_scatter x2 -> x0, waiting for transfers between devices: 3.82 us -> none  [reduced_to_own(): blocks = lax.psum_scatter(blocks, axes[k], scatter_dimension=0, tiled=True)]
  transfers between devices with their start and end apart: 3 -> 0, of which waited for: 2 -> 0; matrix products, arithmetic and copies ran while one was open for 38% -> 0% of each run, Pallas kernels for 0% -> 0%
where the time goes in v1:
time: 60.6 us; the launch traced here: 60.1 us
  Pallas kernels  56.8 us (94%)
  local copies, waits for them, and re-layouts  2.7 us (4%)
  between operations  0.64 us (1%)
    pallas_call x1, Pallas kernels, exchange(): pl.pallas_call(exchange_kernel, in_specs=[pl.BlockSpec(memory_space=pl.AN...  40.4 us
    pallas_call x1, Pallas kernels, pool(): pl.pallas_call(pool_kernel, grid=(tw,), in_specs=[block((1, depth, bags))...  16.4 us
    unnamed x2, local copies, waits for them, and re-layouts  2.7 us

profile of v1, /device:TPU:8, one launch (start us, length us, event | category | flops | bytes accessed | tf_op | source)
XLA Modules:
  0.0 60.1 jit_solution(18349437941718578199)
XLA Ops:
  0.6 16.4 %shard_map.77 = (f32[4,256,8,128]{3,2,1,0:T(8,128)}, f32[2,128,128]{2,1,0:T(8,128)}) custom-call(s32[4,32,2048]{2,1,0:T(8,128)} %wi.1, bf16[4,512,256]{2,1,0:T(8,128)(2,1)} %wt.1, bf16[4,256,128]{2,1,0:T(8,128)(2,1)} %wp.1, s32[8,32,128]{2,1,0:T(8,128)} %ti.1, bf16[8,32,4096]{2,1,0:T(8,128)(2,1)} %tt.1), custom_call_target="tpu_custom_call" | custom-call | tf_op jit(solution)/shard_map/pallas_call | solution.py:188
  17.0 40.4 %shard_map.78 = (f32[8,512]{1,0:T(8,128)}, f32[8,1024]{1,0:T(8,128)}) custom-call(f32[4,2,2,2,2,2,8,8,128]{8,7,6,5,4,3,2,1,0:T(8,128)} %bitcast.3, f32[2,16,8,128]{3,2,1,0:T(8,128)} %bitcast.4, bf16[2,128,128]{2,1,0:T(8,128)(2,1)} %bitcast.5), custom_call_target="tpu_custom_call" | custom-call | tf_op jit(solution)/shard_map/pallas_call | solution.py:345
  57.4 1.3 %copy.10 = f32[8,512]{1,0:T(8,128)} copy(f32[8,512]{1,0:T(8,128)} %get-tuple-element.8) | data formatting | bytes 32768
  58.8 1.4 %copy.11 = f32[8,1024]{1,0:T(8,128)} copy(f32[8,1024]{1,0:T(8,128)} %get-tuple-element.9) | data formatting | bytes 65536

commit v2 on v0

v2 whole, which is shorter than its diff:
```python
import jax
import jax.numpy as jnp
from jax import lax
from jax.experimental import pallas as pl
from jax.experimental.pallas import tpu as pltpu
from jax.sharding import PartitionSpec as P

F32, BF16, I32 = jnp.float32, jnp.bfloat16, jnp.int32
MESH = pl.DeviceIdType.MESH
GX_GY = ("gx", "gy")

WIDE_SLOTS = 4
THIN_SLOTS = 12
BLOCK = 256


def keys_of(index, first, count, axis):
    row = index - first
    place = lax.broadcasted_iota(I32, row.shape, axis)
    return jnp.where((row >= 0) & (row < count), row * 32 + place, -1)


def next_slot(keys, slot, axis=0):
    return jnp.max(jnp.where(keys < slot, keys, -1), axis=axis, keepdims=True)


def mark_of(values):
    return jnp.broadcast_to(values, (16, values.shape[1])).astype(BF16)


def wide_mark(slot):
    return jnp.where(slot < 0, 256, (slot >> 5) - 256).astype(F32)


def ids_of(first):
    return (lax.broadcasted_iota(I32, (16, 128), 0) + first).astype(F32).astype(BF16)


def one_hot(marks, chunk):
    one, zero = jnp.ones((16, 128), BF16), jnp.zeros((16, 128), BF16)
    hit = jnp.where(chunk == marks[0], one, zero)
    for mark in marks[1:]:
        hit = hit + jnp.where(chunk == mark, one, zero)
    return hit


def split_projection(table, weight):
    projected = jnp.dot(table, weight, preferred_element_type=F32).T
    high = projected.astype(BF16)
    low = (projected - high.astype(F32)).astype(BF16)
    return jnp.concatenate([high, low], axis=0)


def place_of(c, y_lo, z, y_hi, x):
    bits = ((x // 2) ^ (x % 2), y_hi ^ y_lo, x // 2, y_hi)
    return sum((8 >> ((d - c + 4) % 4)) * 8 * bits[d] for d in range(4)) + z


def find_kernel(
    wi, ti, wt, wp, tt, wslot, tslot, wextra, textra,
    wkeys, more, hits, proj, extra, wbuf, pbuf, tbuf, lines, low, zsem, sem,
):
    gx, gy = lax.axis_index("gx"), lax.axis_index("gy")
    tables, _, bags = wi.shape
    rows_w, rows_t = wt.shape[1], tt.shape[2]
    first_w, first_t = (gx * 16 + gy) * rows_w, gy * rows_t
    blocks = bags // BLOCK

    extra[...] = jnp.zeros_like(extra)
    fills = [pltpu.make_async_copy(extra, wextra.at[t], zsem.at[t]) for t in range(tables)]
    for fill in fills:
        fill.start()
    textra[...] = jnp.zeros_like(textra)

    left = jnp.full((1, 128), -1, I32)
    for t in range(tables):
        for b in range(blocks):
            at = slice(b * BLOCK, (b + 1) * BLOCK)
            keys = keys_of(wi[t, :, at], first_w, rows_w, 0)
            slot = jnp.max(keys, axis=0, keepdims=True)
            for k in range(WIDE_SLOTS):
                wslot[t, k : k + 1, at] = wide_mark(slot)
                slot = next_slot(keys, slot)
            more[t, :, at] = slot
            for c in range(BLOCK // 128):
                left = jnp.maximum(left, slot[:, c * 128 : c * 128 + 128])
    wide_left = jnp.max(left)

    thin_keys = keys_of(ti[...], first_t, rows_t, 1)
    slot = jnp.max(thin_keys, axis=1, keepdims=True)
    for k in range(THIN_SLOTS):
        tslot[:, k : k + 1, :] = slot >> 5
        slot = next_slot(thin_keys, slot, 1)
    thin_left = jnp.max(slot)
    for fill in fills:
        fill.wait()

    def fetch(src, dst):
        copy = pltpu.make_async_copy(src, dst, sem)
        copy.start()
        copy.wait()

    @pl.when(wide_left >= 0)
    def _():
        wkeys[...] = keys_of(wi[...], first_w, rows_w, 1)

        def table(t, _):
            @pl.when(jnp.max(more[t]) >= 0)
            def _():
                fetch(wt.at[t], wbuf)
                fetch(wp.at[t], pbuf)
                proj[...] = split_projection(wbuf[...], pbuf[...])

                def block(b, _):
                    at = pl.ds(pl.multiple_of(b * BLOCK, BLOCK), BLOCK)
                    top = jnp.max(more[t, :, at])

                    @pl.when(top >= 0)
                    def _():
                        hits[...] = jnp.zeros_like(hits)

                        def body(carry):
                            slot, _ = carry
                            for c in range(BLOCK // 128):
                                mark = mark_of(wide_mark(slot[:, c * 128 : c * 128 + 128]))
                                for r in range(rows_w // 16):
                                    spot = (slice(r * 16, r * 16 + 16), slice(c * 128, c * 128 + 128))
                                    hits[spot] = hits[spot] + one_hot([mark], ids_of(r * 16 - 256))
                            slot = next_slot(wkeys[t, :, at], slot)
                            return slot, jnp.max(slot)

                        lax.while_loop(lambda carry: carry[1] >= 0, body, (more[t, :, at], top))
                        both = jnp.dot(proj[...], hits[...], preferred_element_type=F32)
                        found = (both[:128] + both[128:]).T
                        step = [(8 >> ((d - t + 4) % 4)) * 8 for d in range(4)]
                        for g in range(BLOCK // 128):
                            group = b * (BLOCK // 128) + g
                            y_lo, z = group // 8, group % 8
                            for y_hi in range(2):
                                crossed = (y_hi + y_lo) % 2
                                for x in range(4):
                                    place = z + step[0] * ((x // 2) ^ (x % 2)) + step[1] * crossed
                                    place = place + step[2] * (x // 2) + step[3] * y_hi
                                    for core in range(2):
                                        row = g * 128 + y_hi * 64 + x * 16 + core * 8
                                        extra[core * 128 + place] = found[row : row + 8]

                    return 0

                lax.fori_loop(0, blocks, block, 0)
                fetch(extra, wextra.at[t])
                extra[...] = jnp.zeros_like(extra)

            return 0

        lax.fori_loop(0, tables, table, 0)

    @pl.when(thin_left >= 0)
    def _():
        groups = rows_t // 256

        def table(i, _):
            keys = keys_of(ti[i], first_t, rows_t, 0)
            slot = jnp.max(keys, axis=0, keepdims=True)
            for _ in range(THIN_SLOTS):
                slot = next_slot(keys, slot)
            top = jnp.max(slot)

            @pl.when(top >= 0)
            def _():
                fetch(tt.at[i], tbuf)
                for g in range(groups):
                    lines[g * 32 : g * 32 + 32, :] = tbuf[:, g * 256 : g * 256 + 256]

                def body(carry):
                    slot, _ = carry
                    mark = mark_of(((slot >> 5) & 255).astype(F32))
                    for r in range(16):
                        low[r * 16 : r * 16 + 16, :] = one_hot([mark], ids_of(r * 16))
                    found = jnp.dot(lines[...], low[...], preferred_element_type=F32)
                    group = jnp.broadcast_to(slot >> 13, (32, 128))
                    total = textra[i]
                    for g in range(groups):
                        total = total + jnp.where(group == g, found[g * 32 : g * 32 + 32], 0.0)
                    textra[i] = total
                    slot = next_slot(keys, slot)
                    return slot, jnp.max(slot)

                lax.while_loop(lambda carry: carry[1] >= 0, body, (slot, top))

            return 0

        lax.fori_loop(0, ti.shape[0], table, 0)


def find(wide_index, thin_index, wide_table, wide_proj, thin_table):
    tw, _, bags = wide_index.shape
    tt, _, own_bags = thin_index.shape
    rows_w, ww = wide_table.shape[1:]
    wt, rows_t = thin_table.shape[1:]
    vmem, anywhere = pl.BlockSpec(memory_space=pltpu.VMEM), pl.BlockSpec(memory_space=pl.ANY)
    return pl.pallas_call(
        find_kernel,
        in_specs=[vmem, vmem, anywhere, anywhere, anywhere],
        out_specs=[vmem, vmem, anywhere, vmem],
        out_shape=[
            jax.ShapeDtypeStruct((tw, WIDE_SLOTS, bags), F32),
            jax.ShapeDtypeStruct((tt, THIN_SLOTS, own_bags), I32),
            jax.ShapeDtypeStruct((tw, bags // 8, 8, 128), F32),
            jax.ShapeDtypeStruct((tt, wt, own_bags), F32),
        ],
        scratch_shapes=[
            pltpu.VMEM(wide_index.shape, I32),
            pltpu.VMEM((tw, 1, bags), I32),
            pltpu.VMEM((rows_w, BLOCK), BF16),
            pltpu.VMEM((256, rows_w), BF16),
            pltpu.VMEM((bags // 8, 8, 128), F32),
            pltpu.VMEM((rows_w, ww), BF16),
            pltpu.VMEM((ww, 128), BF16),
            pltpu.VMEM((wt, rows_t), BF16),
            pltpu.VMEM((rows_t // 256 * wt, 256), BF16),
            pltpu.VMEM((256, 128), BF16),
            pltpu.SemaphoreType.DMA((tw,)),
            pltpu.SemaphoreType.DMA,
        ],
        compiler_params=pltpu.CompilerParams(),
    )(wide_index, thin_index, wide_table, wide_proj, thin_table)


def pool_kernel(
    wslot, tslot, textra, pj, wextra, wt, wp, tt, out,
    part, wbuf, pbuf, tbuf, sums, th, r0, r1, r2, rm, r4, rz, rt,
    esem, wsem, psem, tsem, ssem, rsem, ms, mr, zs, zr, ts, tr,
):
    gx, gy = lax.axis_index("gx"), lax.axis_index("gy")
    y_lo, z = gx // 8, gx % 8
    y_hi, x, core = gy // 8, (gy // 2) % 4, gy % 2

    def device(flip_lo, y_hi, x, core=core):
        return ((1 - y_lo if flip_lo else y_lo) * 8 + z, y_hi * 8 + x * 2 + core)

    moves = [
        (False, y_hi, x + 1 - 2 * (x % 2), (x // 2 + x % 2) % 2),
        (True, y_hi, x, (y_hi + y_lo) % 2),
        (False, y_hi, 3 - x, x // 2),
        (True, 1 - y_hi, x, y_hi),
    ]
    links = [device(*move[:3]) for move in moves]
    bits = [[moves[(c + k) % 4][3] for k in range(4)] for c in range(4)]
    partners = [[links[(c + k) % 4] for k in range(4)] for c in range(4)]
    corners = []
    for c in range(4):
        a, b = moves[(c + 2) % 4], moves[(c + 3) % 4]
        along_x, along_y = (a, b) if c % 2 == 0 else (b, a)
        corners.append(device(True, along_y[1], along_x[2]))
    other = device(False, y_hi, x, 1 - core)
    along_z = [None] + [(y_lo * 8 + (z + d) % 8, gy) for d in range(1, 8)]
    along_gy = [None] + [(gx, (gy + d) % 16) for d in range(1, 16)]

    barrier = pltpu.get_barrier_semaphore()
    peers = along_gy[1:] + along_z[1:] + [links[1], links[3]] + corners
    for peer in peers:
        pl.semaphore_signal(barrier, inc=1, device_id=peer, device_id_type=MESH)

    weights = pltpu.make_async_copy(wp, pbuf, psem)
    weights.start()
    tables = [pltpu.make_async_copy(wt.at[c], wbuf.at[c], wsem.at[c]) for c in range(4)]
    extras = [pltpu.make_async_copy(wextra.at[c], part.at[c], esem.at[c]) for c in range(4)]
    for c in range(4):
        tables[c].start()
        extras[c].start()
    thin_rows = pltpu.make_async_copy(tt, tbuf, tsem)
    thin_rows.start()

    def send(src, dst, s, r, to):
        copy = pltpu.make_async_remote_copy(
            src_ref=src, dst_ref=dst, send_sem=s, recv_sem=r, device_id=to, device_id_type=MESH
        )
        copy.start()
        return copy

    def wide_part(c):
        tables[c].wait()
        if c == 0:
            weights.wait()
        both_parts = split_projection(wbuf[c], pbuf[c])
        rows = wbuf.shape[1]
        chunks = [ids_of(r * 16 - 256) for r in range(rows // 16)]
        extras[c].wait()
        for b in range(wslot.shape[2] // BLOCK):
            columns = []
            for g in range(BLOCK // 128):
                at = b * BLOCK + g * 128
                marks = [mark_of(wslot[c, k : k + 1, at : at + 128]) for k in range(WIDE_SLOTS)]
                columns.append(jnp.concatenate([one_hot(marks, chunk) for chunk in chunks], axis=0))
            hits = jnp.concatenate(columns, axis=1)
            both = jnp.dot(both_parts, hits, preferred_element_type=F32)
            found = (both[:128] + both[128:]).T
            for g in range(BLOCK // 128):
                g_lo, g_z = divmod(b * (BLOCK // 128) + g, 8)
                for g_hi in range(2):
                    for g_x in range(4):
                        place = place_of(c, g_lo, g_z, g_hi, g_x)
                        for g_core in range(2):
                            row = g * 128 + g_hi * 64 + g_x * 16 + g_core * 8
                            spot = (c, g_core, place // 8, place % 8)
                            part[spot] = part[spot] + found[row : row + 8]

    def thin_table(i, _):
        groups = tbuf.shape[2] // 256
        lines = jnp.concatenate([tbuf[i, :, g * 256 : g * 256 + 256] for g in range(groups)], axis=0)
        chunks = [ids_of(r * 16) for r in range(16)]
        total = [textra[i, f * 8 : f * 8 + 8, :] for f in range(4)]
        for pair in range(THIN_SLOTS // 2):
            slots = [tslot[i, pair * 2 + k : pair * 2 + k + 1, :] for k in range(2)]
            columns = []
            for slot in slots:
                mark = mark_of((slot & 255).astype(F32))
                columns.append(jnp.concatenate([one_hot([mark], chunk) for chunk in chunks], axis=0))
            low = jnp.concatenate(columns, axis=1)
            found = jnp.dot(lines, low, preferred_element_type=F32)
            for k in range(2):
                group = jnp.broadcast_to(slots[k] >> 8, (8, 128))
                picked = [jnp.zeros((8, 128), F32)] * 4
                for g in range(groups):
                    same = group == g
                    for f in range(4):
                        row = g * 32 + f * 8
                        piece = found[row : row + 8, k * 128 : k * 128 + 128]
                        picked[f] = jnp.where(same, piece, picked[f])
                total = [a + b for a, b in zip(total, picked)]
        for f in range(4):
            sums[pl.ds(pl.multiple_of(i * 32 + f * 8, 8), 8), :] = total[f]
        return 0

    sends = []
    halves = [None] * 4
    first = [None] * 4

    def step_first(c):
        halves[c].wait_recv()
        sends.append(halves[c])
        go, stay = 1 - bits[c][0], bits[c][0]
        for side in (go, stay):
            half = pl.ds(side * 8, 8)
            part[c, core, half] = part[c, core, half] + r0[c, half]
            if side is go:
                first[c] = send(
                    part.at[c, core, half], r1.at[c], ssem.at[1, c], rsem.at[1, c], partners[c][0]
                )

    for c in range(4):
        wide_part(c)
        if c == 0:
            pl.semaphore_wait(barrier, len(peers))
        halves[c] = send(
            part.at[c, 1 - core], r0.at[c], ssem.at[0, c], rsem.at[0, c], other
        )
        if c > 0:
            step_first(c - 1)
    step_first(3)

    thin_rows.wait()
    lax.fori_loop(0, tbuf.shape[0], thin_table, 0)
    for h in range(2):
        th[h] = sums[h * 128 : h * 128 + 128, :].T.reshape(16, 8, 128)

    second = []
    for c in range(4):
        first[c].wait_recv()
        sends.append(first[c])
        kept, go, stay = bits[c][0], 1 - bits[c][1], bits[c][1]
        for side in (go, stay):
            half = pl.ds(side * 4, 4)
            r1[c, half] = r1[c, half] + part[c, core, pl.ds(kept * 8 + side * 4, 4)]
            if side is go:
                second.append(
                    send(r1.at[c, half], r2.at[c], ssem.at[2, c], rsem.at[2, c], partners[c][1])
                )
    thins = []
    for d in range(1, 16):
        thins.append(send(th.at[:, along_gy[d][1]], rt.at[d], ts.at[d], tr.at[d], along_gy[d]))

    thirds = []
    for c in range(4):
        second[c].wait_recv()
        sends.append(second[c])
        kept, (b2, b3) = bits[c][1], bits[c][2:]
        ways = [
            (1 - b2, 1 - b3, corners[c]),
            (1 - b2, b3, partners[c][2]),
            (b2, 1 - b3, partners[c][3]),
        ]
        row = []
        for j, (i2, i3, to) in enumerate(ways):
            here = i2 * 2 + i3
            r2[c, here] = r2[c, here] + r1[c, kept * 4 + here]
            row.append(send(r2.at[c, here], rm.at[c, j], ms.at[c, j], mr.at[c, j], to))
        thirds.append(row)

    for c in range(4):
        here = bits[c][2] * 2 + bits[c][3]
        total = r2[c, here] + r1[c, bits[c][1] * 4 + here]
        for j in range(3):
            thirds[c][j].wait_recv()
            sends.append(thirds[c][j])
            total = total + rm[c, j]
        r4[c] = total
    lasts = []
    for d in (4, 3, 5, 2, 6, 1, 7):
        lasts.append(
            (d, send(r4.at[:, (z + d) % 8], rz.at[d], zs.at[d], zr.at[d], along_z[d]))
        )

    for copy in thins:
        copy.wait_recv()
    pooled = th[:, gy]
    for d in range(1, 16):
        pooled = pooled + rt[d]
    group = lax.broadcasted_iota(I32, (8, 128), 1) // 32
    for h in range(2):
        rows = jnp.concatenate([jnp.where(group == g, pooled[h], 0.0) for g in range(4)], axis=0)
        projected = jnp.dot(
            rows, pj[h].astype(F32), preferred_element_type=F32, precision=lax.Precision.HIGHEST
        )
        for g in range(4):
            at = 512 + (h * 4 + g) * 128
            out[:, at : at + 128] = projected[g * 8 : g * 8 + 8]

    total = r4[:, z]
    for d, copy in lasts:
        copy.wait_recv()
        total = total + rz[d]
    for c in range(4):
        out[:, c * 128 : c * 128 + 128] = total[c]
    for copy in sends + thins + [copy for _, copy in lasts]:
        copy.wait_send()


def pool(wslot, tslot, wextra, textra, wide_table, wide_proj, thin_table, thin_proj):
    vmem, anywhere = pl.BlockSpec(memory_space=pltpu.VMEM), pl.BlockSpec(memory_space=pl.ANY)
    dma = pltpu.SemaphoreType.DMA
    return pl.pallas_call(
        pool_kernel,
        in_specs=[vmem] * 4 + [anywhere] * 4,
        out_specs=vmem,
        out_shape=jax.ShapeDtypeStruct((8, 1536), F32),
        scratch_shapes=[
            pltpu.VMEM((4, 2, 16, 8, 8, 128), F32),
            pltpu.VMEM(wide_table.shape, BF16),
            pltpu.VMEM(wide_proj.shape, BF16),
            pltpu.VMEM(thin_table.shape, BF16),
            pltpu.VMEM((256, 128), F32),
            pltpu.VMEM((2, 16, 8, 128), F32),
            pltpu.VMEM((4, 16, 8, 8, 128), F32),
            pltpu.VMEM((4, 8, 8, 8, 128), F32),
            pltpu.VMEM((4, 4, 8, 8, 128), F32),
            pltpu.VMEM((4, 3, 8, 8, 128), F32),
            pltpu.VMEM((4, 8, 8, 128), F32),
            pltpu.VMEM((8, 4, 8, 128), F32),
            pltpu.VMEM((16, 2, 8, 128), F32),
            dma((4,)),
            dma((4,)),
            dma,
            dma,
            dma((3, 4)),
            dma((3, 4)),
            dma((4, 3)),
            dma((4, 3)),
            dma((8,)),
            dma((8,)),
            dma((16,)),
            dma((16,)),
        ],
        compiler_params=pltpu.CompilerParams(collective_id=0, has_side_effects=True),
    )(
        wslot, tslot, textra, thin_proj.reshape(2, 128, 128),
        wextra.reshape(4, 2, 16, 8, 8, 128), wide_table, wide_proj, thin_table,
    )


def local(wide_index, wide_table, wide_proj, thin_index, thin_table, thin_proj):
    wslot, tslot, wextra, textra = find(wide_index, thin_index, wide_table, wide_proj, thin_table)
    out = pool(wslot, tslot, wextra, textra, wide_table, wide_proj, thin_table, thin_proj)
    return out[:, :512], out[:, 512:]


def solution(mesh):
    placed = (P(), P(None, GX_GY, None), P(), P(None, None, "gx"), P(None, None, "gy"), P())
    return jax.shard_map(
        local,
        mesh=mesh,
        in_specs=placed,
        out_specs=(P(GX_GY, None), P(GX_GY, None)),
        check_vma=False,
    )
```

time: 257 us -> 53.4 us (0.21)
  other arithmetic: 153 us -> 0 us
  Pallas kernels: 0 us -> 49.8 us
  matrix products: 33 us -> 0 us
  blocking collectives: 18.3 us -> 0 us
  local copies, waits for them, and re-layouts: 16.6 us -> 2.7 us
  between operations: 14.3 us -> 0.65 us
  waiting for transfers between devices: 12.6 us -> 0 us
  starting transfers between devices: 5.57 us -> 0 us
    reduce_sum x22 -> x0, other arithmetic: 150 us -> none  [the longest x20 148 us: hit_counts(): jnp.sum((block_index[:, :, None] == row_ids[None, None, :]).astype(jnp.bf...]
    pallas_call x0 -> x2, Pallas kernels: none -> 49.8 us  [the longest x1 43.9 us: pool(): pl.pallas_call(pool_kernel, in_specs=[vmem] * 4 + [anywhere] * 4, out_spe...]
    dot_general x36 -> x0, matrix products: 33 us -> none  [the longest x12 13.8 us: project(): jnp.dot(pooled, weight.astype(jnp.float32), precision=lax.Precision.HIGHEST)]
    all_to_all x1 -> x0, blocking collectives: 18.3 us -> none  [summed_on_arrival(): blocks = lax.all_to_all(split_up(shard, dim, count), axis, 0, 0, tiled=True)]
    another operation x9 -> x0, local copies, waits for them, and re-layouts: 10.9 us -> none  [the longest x1 5.31 us: reduced_to_own(): blocks = blocks.reshape(*dims, *blocks.shape[1:])]
    all_to_all x1 -> x0, waiting for transfers between devices: 8.7 us -> none  [summed_on_arrival(): blocks = lax.all_to_all(split_up(shard, dim, count), axis, 0, 0, tiled=True)]
    all_to_all x1 -> x0, starting transfers between devices: 5.31 us -> none  [summed_on_arrival(): blocks = lax.all_to_all(split_up(shard, dim, count), axis, 0, 0, tiled=True)]
    reduce_scatter x2 -> x0, waiting for transfers between devices: 3.82 us -> none  [reduced_to_own(): blocks = lax.psum_scatter(blocks, axes[k], scatter_dimension=0, tiled=True)]
  transfers between devices with their start and end apart: 3 -> 0, of which waited for: 2 -> 0; matrix products, arithmetic and copies ran while one was open for 38% -> 0% of each run, Pallas kernels for 0% -> 0%
where the time goes in v2:
time: 53.4 us; the launch traced here: 53.1 us
  Pallas kernels  49.8 us (93%)
  local copies, waits for them, and re-layouts  2.7 us (5%)
  between operations  0.65 us (1%)
    pallas_call x1, Pallas kernels, pool(): pl.pallas_call(pool_kernel, in_specs=[vmem] * 4 + [anywhere] * 4, out_spe...  43.9 us
    pallas_call x1, Pallas kernels, find(): pl.pallas_call(find_kernel, in_specs=[vmem, vmem, anywhere, anywhere, any...  5.83 us
    slice x2, local copies, waits for them, and re-layouts, local(): return (out[:, :512], out[:, 512:])  2.7 us

profile of v2, /device:TPU:8, one launch (start us, length us, event | category | flops | bytes accessed | tf_op | source)
XLA Modules:
  0.0 53.1 jit_solution(17102885467409054524)
XLA Ops:
  0.6 5.8 %shard_map.77 = (f32[4,4,2048]{2,1,0:T(4,128)}, s32[8,12,128]{2,1,0:T(8,128)}, f32[4,256,8,128]{3,2,1,0:T(8,128)}, f32[8,32,128]{2,1,0:T(8,128)}) custom-call(s32[4,32,2048]{2,1,0:T(8,128)} %wi.1, s32[8,32,128]{2,1,0:T(8,128)} %ti.1, bf16[4,512,256]{2,1,0:T(8,128)(2,1)} %wt.3, bf16[4,256,128]{2,1,0:T(8,128)(2,1)} %wp.3, bf16[8,32,4096]{2,1,0:T(8,128)(2,1)} %tt.3), custom_call_target="tpu_custom_call" | custom-call | tf_op jit(solution)/shard_map/pallas_call | solution.py:202
  6.5 43.9 %shard_map.78 = f32[8,1536]{1,0:T(8,128)} custom-call(f32[4,4,2048]{2,1,0:T(4,128)} %get-tuple-element.6.wslot, s32[8,12,128]{2,1,0:T(8,128)} %get-tuple-element.7.tslot, f32[8,32,128]{2,1,0:T(8,128)} %get-tuple-element.8.textra, bf16[2,128,128]{2,1,0:T(8,128)(2,1)} %bitcast.3, f32[4,2,16,8,8,128]{5,4,3,2,1,0:T(8,128)} %bitcast.2, bf16[4,512,256]{2,1,0:T(8,128)(2,1)} %wt.3, ...), custom_call_target="tpu_custom_call" | custom-call | tf_op jit(solution)/shard_map/pallas_call | solution.py:443
  50.4 1.3 %slice.6 = f32[8,512]{1,0:T(8,128)} slice(f32[8,1536]{1,0:T(8,128)} %shard_map.78), slice={[0:8], [0:512]} | slice | bytes 32768 | tf_op jit(solution)/shard_map/slice | solution.py:485
  51.7 1.4 %slice.7 = f32[8,1024]{1,0:T(8,128)} slice(f32[8,1536]{1,0:T(8,128)} %shard_map.78), slice={[0:8], [512:1536]} | slice | bytes 65536 | tf_op jit(solution)/shard_map/slice | solution.py:485

commit v3 on v2

v3 whole, which is shorter than its diff:
```python
import functools

import jax
import jax.numpy as jnp
from jax import lax
from jax.experimental import pallas as pl
from jax.experimental.pallas import tpu as pltpu
from jax.sharding import PartitionSpec as P

F32, BF16, I32 = jnp.float32, jnp.bfloat16, jnp.int32
MESH = pl.DeviceIdType.MESH
GX_GY = ("gx", "gy")

WIDE_SLOTS = 4
THIN_SLOTS = 12
BLOCK = 256


def keys_of(index, first, count, axis):
    row = index - first
    place = lax.broadcasted_iota(I32, row.shape, axis)
    return jnp.where((row >= 0) & (row < count), row * 32 + place, -1)


def next_slot(keys, slot, axis=0):
    return jnp.max(jnp.where(keys < slot, keys, -1), axis=axis, keepdims=True)


def mark_of(values):
    return jnp.broadcast_to(values, (16, values.shape[1])).astype(BF16)


def wide_mark(slot):
    return jnp.where(slot < 0, 256, (slot >> 5) - 256).astype(F32)


def ids_of(first):
    return (lax.broadcasted_iota(I32, (16, 128), 0) + first).astype(F32).astype(BF16)


def one_hot(marks, chunk):
    one, zero = jnp.ones((16, 128), BF16), jnp.zeros((16, 128), BF16)
    hit = jnp.where(chunk == marks[0], one, zero)
    for mark in marks[1:]:
        hit = hit + jnp.where(chunk == mark, one, zero)
    return hit


def split_projection(table, weight):
    projected = jnp.dot(table, weight, preferred_element_type=F32).T
    high = projected.astype(BF16)
    low = (projected - high.astype(F32)).astype(BF16)
    return jnp.concatenate([high, low], axis=0)


def place_of(q, y_lo, y_hi, x):
    bits = ((x // 2) ^ (x % 2), y_hi ^ y_lo, x // 2, y_hi)
    return sum((8 >> ((d - q) % 4)) * bits[d] for d in range(4))


def find_kernel(rows_w, rows_t, wi, ti, wslot, tslot, wmore, tmore, left):
    gx, gy = lax.axis_index("gx"), lax.axis_index("gy")
    tables, _, bags = wi.shape
    first_w, first_t = (gx * 16 + gy) * rows_w, gy * rows_t

    most = jnp.full((1, 128), -1, I32)
    for t in range(tables):
        for b in range(bags // BLOCK):
            at = slice(b * BLOCK, (b + 1) * BLOCK)
            keys = keys_of(wi[t, :, at], first_w, rows_w, 0)
            slot = jnp.max(keys, axis=0, keepdims=True)
            for k in range(WIDE_SLOTS):
                wslot[t, k : k + 1, at] = wide_mark(slot)
                slot = next_slot(keys, slot)
            wmore[t, :, at] = slot
            for c in range(BLOCK // 128):
                most = jnp.maximum(most, slot[:, c * 128 : c * 128 + 128])
    left[0] = jnp.broadcast_to(most, (8, 128))

    thin_keys = keys_of(ti[...], first_t, rows_t, 1)
    slot = jnp.max(thin_keys, axis=1, keepdims=True)
    for k in range(THIN_SLOTS):
        tslot[:, k : k + 1, :] = slot >> 5
        slot = next_slot(thin_keys, slot, 1)
    tmore[...] = slot
    left[1] = jnp.broadcast_to(jnp.max(slot, axis=0), (8, 128))


def spill_kernel(
    wi, ti, wmore, tmore, left, wt, wp, tt, wextra, textra,
    wkeys, hits, proj, lines, low,
):
    gx, gy = lax.axis_index("gx"), lax.axis_index("gy")
    tables, _, bags = wi.shape
    rows_w, rows_t = wt.shape[1], tt.shape[2]
    first_w, first_t = (gx * 16 + gy) * rows_w, gy * rows_t
    blocks = bags // BLOCK
    wextra[...] = jnp.zeros_like(wextra)
    textra[...] = jnp.zeros_like(textra)
    wide_left, thin_left = jnp.max(left[0]), jnp.max(left[1])

    @pl.when(wide_left >= 0)
    def _():
        wkeys[...] = keys_of(wi[...], first_w, rows_w, 1)

        def table(t, _):
            @pl.when(jnp.max(wmore[t]) >= 0)
            def _():
                proj[...] = split_projection(wt[t], wp[t])

                def block(b, _):
                    at = pl.ds(pl.multiple_of(b * BLOCK, BLOCK), BLOCK)
                    top = jnp.max(wmore[t, :, at])

                    @pl.when(top >= 0)
                    def _():
                        hits[...] = jnp.zeros_like(hits)

                        def body(carry):
                            slot, _ = carry
                            for c in range(BLOCK // 128):
                                mark = mark_of(wide_mark(slot[:, c * 128 : c * 128 + 128]))
                                for r in range(rows_w // 16):
                                    spot = (slice(r * 16, r * 16 + 16), slice(c * 128, c * 128 + 128))
                                    hits[spot] = hits[spot] + one_hot([mark], ids_of(r * 16 - 256))
                            slot = next_slot(wkeys[t, :, at], slot)
                            return slot, jnp.max(slot)

                        lax.while_loop(lambda carry: carry[1] >= 0, body, (wmore[t, :, at], top))
                        both = jnp.dot(proj[...], hits[...], preferred_element_type=F32)
                        found = (both[:128] + both[128:]).T
                        for g in range(BLOCK // 128):
                            group = b * (BLOCK // 128) + g
                            y_lo, z = group // 8, group % 8
                            quarter = z // 2
                            step = [8 >> ((d - quarter + 4) % 4) for d in range(4)]
                            for y_hi in range(2):
                                crossed = (y_hi + y_lo) % 2
                                for x in range(4):
                                    place = step[0] * ((x // 2) ^ (x % 2)) + step[1] * crossed
                                    place = place + step[2] * (x // 2) + step[3] * y_hi
                                    place = quarter * 32 + place * 2 + z % 2
                                    for core in range(2):
                                        row = g * 128 + y_hi * 64 + x * 16 + core * 8
                                        wextra[t, core * 128 + place] = found[row : row + 8]

                    return 0

                lax.fori_loop(0, blocks, block, 0)

            return 0

        lax.fori_loop(0, tables, table, 0)

    @pl.when(thin_left >= 0)
    def _():
        groups = rows_t // 256

        def table(i, _):
            keys = keys_of(ti[i], first_t, rows_t, 0)
            slot = tmore[i]
            top = jnp.max(slot)

            @pl.when(top >= 0)
            def _():
                for g in range(groups):
                    lines[g * 32 : g * 32 + 32, :] = tt[i, :, g * 256 : g * 256 + 256]

                def body(carry):
                    slot, _ = carry
                    mark = mark_of(((slot >> 5) & 255).astype(F32))
                    for r in range(16):
                        low[r * 16 : r * 16 + 16, :] = one_hot([mark], ids_of(r * 16))
                    found = jnp.dot(lines[...], low[...], preferred_element_type=F32)
                    group = jnp.broadcast_to(slot >> 13, (32, 128))
                    total = textra[i]
                    for g in range(groups):
                        total = total + jnp.where(group == g, found[g * 32 : g * 32 + 32], 0.0)
                    textra[i] = total
                    slot = next_slot(keys, slot)
                    return slot, jnp.max(slot)

                lax.while_loop(lambda carry: carry[1] >= 0, body, (slot, top))

            return 0

        lax.fori_loop(0, ti.shape[0], table, 0)


def find(wide_index, thin_index, wide_table, wide_proj, thin_table):
    tw, _, bags = wide_index.shape
    tt, _, own_bags = thin_index.shape
    rows_w = wide_table.shape[1]
    wt, rows_t = thin_table.shape[1:]
    vmem = pl.BlockSpec(memory_space=pltpu.VMEM)
    params = pltpu.CompilerParams(vmem_limit_bytes=16 * 2**20)
    wslot, tslot, wmore, tmore, left = pl.pallas_call(
        functools.partial(find_kernel, rows_w, rows_t),
        in_specs=[vmem] * 2,
        out_specs=[vmem] * 5,
        out_shape=[
            jax.ShapeDtypeStruct((tw, WIDE_SLOTS, bags), F32),
            jax.ShapeDtypeStruct((tt, THIN_SLOTS, own_bags), I32),
            jax.ShapeDtypeStruct((tw, 1, bags), I32),
            jax.ShapeDtypeStruct((tt, 1, own_bags), I32),
            jax.ShapeDtypeStruct((2, 8, 128), I32),
        ],
        compiler_params=params,
        cost_estimate=pl.CostEstimate(flops=4 * 10**9, bytes_accessed=1 << 20, transcendentals=0),
    )(wide_index, thin_index)
    wextra, textra = pl.pallas_call(
        spill_kernel,
        in_specs=[vmem] * 8,
        out_specs=[vmem] * 2,
        out_shape=[
            jax.ShapeDtypeStruct((tw, bags // 8, 8, 128), F32),
            jax.ShapeDtypeStruct((tt, wt, own_bags), F32),
        ],
        scratch_shapes=[
            pltpu.VMEM(wide_index.shape, I32),
            pltpu.VMEM((rows_w, BLOCK), BF16),
            pltpu.VMEM((256, rows_w), BF16),
            pltpu.VMEM((rows_t // 256 * wt, 256), BF16),
            pltpu.VMEM((256, 128), BF16),
        ],
        compiler_params=params,
    )(wide_index, thin_index, wmore, tmore, left, wide_table, wide_proj, thin_table)
    return wslot, tslot, wextra, textra


def pool_kernel(
    wslot, tslot, wextra, textra, wt, wp, tt, pj, out,
    part, sums, th, r0, r1, r2, rm, r4, rz, rt,
    hs, hr, ss, sr, ms, mr, zs, zr, ts, tr,
):
    gx, gy = lax.axis_index("gx"), lax.axis_index("gy")
    y_lo, z = gx // 8, gx % 8
    y_hi, x, core = gy // 8, (gy // 2) % 4, gy % 2
    every = range(4)

    def device(flip_lo, y_hi, x, core=core):
        return ((1 - y_lo if flip_lo else y_lo) * 8 + z, y_hi * 8 + x * 2 + core)

    moves = [
        (False, y_hi, x + 1 - 2 * (x % 2), (x // 2 + x % 2) % 2),
        (True, y_hi, x, (y_hi + y_lo) % 2),
        (False, y_hi, 3 - x, x // 2),
        (True, 1 - y_hi, x, y_hi),
    ]
    links = [device(*move[:3]) for move in moves]
    bits = [[moves[(q + k) % 4][3] for k in every] for q in every]
    partners = [[links[(q + k) % 4] for k in every] for q in every]
    corners = []
    for q in every:
        a, b = moves[(q + 2) % 4], moves[(q + 3) % 4]
        along_x, along_y = (a, b) if q % 2 == 0 else (b, a)
        corners.append(device(True, along_y[1], along_x[2]))
    other = device(False, y_hi, x, 1 - core)
    along_z = [None] + [(y_lo * 8 + (z + d) % 8, gy) for d in range(1, 8)]
    along_gy = [None] + [(gx, (gy + d) % 16) for d in range(1, 16)]

    barrier = pltpu.get_barrier_semaphore()
    peers = along_gy[1:] + along_z[1:] + [links[1], links[3]] + corners
    for peer in peers:
        pl.semaphore_signal(barrier, inc=1, device_id=peer, device_id_type=MESH)

    sends = []

    def send(src, dst, s, r, to):
        copy = pltpu.make_async_remote_copy(
            src_ref=src, dst_ref=dst, send_sem=s, recv_sem=r, device_id=to, device_id_type=MESH
        )
        copy.start()
        sends.append(copy)
        return copy

    def wide_part(c):
        both_parts = split_projection(wt[c], wp[c])
        chunks = [ids_of(r * 16 - 256) for r in range(wt.shape[1] // 16)]
        for b in range(wslot.shape[2] // BLOCK):
            columns = []
            for g in range(BLOCK // 128):
                at = b * BLOCK + g * 128
                marks = [mark_of(wslot[c, k : k + 1, at : at + 128]) for k in range(WIDE_SLOTS)]
                columns.append(jnp.concatenate([one_hot(marks, chunk) for chunk in chunks], axis=0))
            hits = jnp.concatenate(columns, axis=1)
            both = jnp.dot(both_parts, hits, preferred_element_type=F32)
            found = (both[:128] + both[128:]).T
            for g in range(BLOCK // 128):
                g_lo, g_z = divmod(b * (BLOCK // 128) + g, 8)
                for g_hi in range(2):
                    for g_x in every:
                        place = place_of(g_z // 2, g_lo, g_hi, g_x)
                        for g_core in range(2):
                            row = g * 128 + g_hi * 64 + g_x * 16 + g_core * 8
                            spot = (c, g_core, g_z // 2, place, g_z % 2)
                            part[spot] = wextra[spot] + found[row : row + 8]

    def thin_table(i, _):
        groups = tt.shape[2] // 256
        lines = jnp.concatenate([tt[i, :, g * 256 : g * 256 + 256] for g in range(groups)], axis=0)
        chunks = [ids_of(r * 16) for r in range(16)]
        total = [textra[i, f * 8 : f * 8 + 8, :] for f in every]
        for pair in range(THIN_SLOTS // 2):
            slots = [tslot[i, pair * 2 + k : pair * 2 + k + 1, :] for k in range(2)]
            columns = []
            for slot in slots:
                mark = mark_of((slot & 255).astype(F32))
                columns.append(jnp.concatenate([one_hot([mark], chunk) for chunk in chunks], axis=0))
            low = jnp.concatenate(columns, axis=1)
            found = jnp.dot(lines, low, preferred_element_type=F32)
            for k in range(2):
                group = jnp.broadcast_to(slots[k] >> 8, (8, 128))
                picked = [jnp.zeros((8, 128), F32)] * 4
                for g in range(groups):
                    same = group == g
                    for f in every:
                        row = g * 32 + f * 8
                        piece = found[row : row + 8, k * 128 : k * 128 + 128]
                        picked[f] = jnp.where(same, piece, picked[f])
                total = [a + b for a, b in zip(total, picked)]
        for f in every:
            sums[pl.ds(pl.multiple_of(i * 32 + f * 8, 8), 8), :] = total[f]
        return 0

    halves, first, second, third, lasts = {}, {}, {}, {}, {}

    def send_half(c):
        halves[c] = send(part.at[c, 1 - core], r0.at[c], hs.at[c], hr.at[c], other)

    def send_first(c):
        halves[c].wait_recv()
        for turn in range(2):
            for q in every:
                half = pl.ds((1 - bits[q][0] if turn == 0 else bits[q][0]) * 8, 8)
                part[c, core, q, half] = part[c, core, q, half] + r0[c, q, half]
                if turn == 0:
                    first[c, q] = send(
                        part.at[c, core, q, half], r1.at[c, q], ss.at[0, c, q], sr.at[0, c, q],
                        partners[q][0],
                    )

    def send_second(c):
        for q in every:
            first[c, q].wait_recv()
            side = 1 - bits[q][1]
            half = pl.ds(side * 4, 4)
            r1[c, q, half] = r1[c, q, half] + part[c, core, q, pl.ds(bits[q][0] * 8 + side * 4, 4)]
            second[c, q] = send(
                r1.at[c, q, half], r2.at[c, q], ss.at[1, c, q], sr.at[1, c, q], partners[q][1]
            )
        for q in every:
            side = bits[q][1]
            half = pl.ds(side * 4, 4)
            r1[c, q, half] = r1[c, q, half] + part[c, core, q, pl.ds(bits[q][0] * 8 + side * 4, 4)]

    def send_third(c):
        for q in every:
            second[c, q].wait_recv()
            b1, b2, b3 = bits[q][1:]
            ways = [
                (1 - b2, 1 - b3, corners[q]),
                (1 - b2, b3, partners[q][2]),
                (b2, 1 - b3, partners[q][3]),
            ]
            for j, (i2, i3, to) in enumerate(ways):
                here = i2 * 2 + i3
                r2[c, q, here] = r2[c, q, here] + r1[c, q, b1 * 4 + here]
                third[c, q, j] = send(
                    r2.at[c, q, here], rm.at[c, q, j], ms.at[c, q, j], mr.at[c, q, j], to
                )

    def send_last(c):
        for q in every:
            b1, b2, b3 = bits[q][1:]
            here = b2 * 2 + b3
            total = r2[c, q, here] + r1[c, q, b1 * 4 + here]
            for j in (1, 2, 0):
                third[c, q, j].wait_recv()
                total = total + rm[c, q, j]
            r4[c, q * 2 : q * 2 + 2] = total
        for d in (4, 3, 5, 2, 6, 1, 7):
            lasts[c, d] = send(
                r4.at[c, (z + d) % 8], rz.at[d, c], zs.at[d, c], zr.at[d, c], along_z[d]
            )

    def thin_tables(begin, end):
        lax.fori_loop(begin, end, thin_table, 0)

    wide_part(0)
    pl.semaphore_wait(barrier, len(peers))
    send_half(0)
    wide_part(1)
    send_half(1)
    wide_part(2)
    send_half(2)
    send_first(0)
    wide_part(3)
    send_half(3)
    send_first(1)
    thin_tables(0, 2)
    send_first(2)
    send_second(0)
    thin_tables(2, 4)
    send_first(3)
    send_second(1)
    thin_tables(4, 6)
    send_second(2)
    send_third(0)
    thin_tables(6, 8)
    for h in range(2):
        th[h] = sums[h * 128 : h * 128 + 128, :].T.reshape(16, 8, 128)
    thins = []
    for d in range(1, 16):
        thins.append(send(th.at[:, along_gy[d][1]], rt.at[d], ts.at[d], tr.at[d], along_gy[d]))
    send_second(3)
    send_third(1)
    send_last(0)
    send_third(2)
    send_last(1)
    send_third(3)
    send_last(2)

    for copy in thins:
        copy.wait_recv()
    pooled = th[:, gy]
    for d in range(1, 16):
        pooled = pooled + rt[d]
    group = lax.broadcasted_iota(I32, (8, 128), 1) // 32
    for h in range(2):
        rows = jnp.concatenate([jnp.where(group == g, pooled[h], 0.0) for g in every], axis=0)
        projected = jnp.dot(
            rows, pj[h].astype(F32), preferred_element_type=F32, precision=lax.Precision.HIGHEST
        )
        for g in every:
            at = 512 + (h * 4 + g) * 128
            out[:, at : at + 128] = projected[g * 8 : g * 8 + 8]

    send_last(3)
    for c in every:
        total = r4[c, z]
        for d in (1, 7, 2, 6, 3, 5, 4):
            lasts[c, d].wait_recv()
            total = total + rz[d, c]
        out[:, c * 128 : c * 128 + 128] = total
    for copy in sends:
        copy.wait_send()


def pool(wslot, tslot, wextra, textra, wide_table, wide_proj, thin_table, thin_proj):
    vmem = pl.BlockSpec(memory_space=pltpu.VMEM)
    dma = pltpu.SemaphoreType.DMA
    return pl.pallas_call(
        pool_kernel,
        in_specs=[vmem] * 8,
        out_specs=vmem,
        out_shape=jax.ShapeDtypeStruct((8, 1536), F32),
        scratch_shapes=[
            pltpu.VMEM((4, 2, 4, 16, 2, 8, 128), F32),
            pltpu.VMEM((256, 128), F32),
            pltpu.VMEM((2, 16, 8, 128), F32),
            pltpu.VMEM((4, 4, 16, 2, 8, 128), F32),
            pltpu.VMEM((4, 4, 8, 2, 8, 128), F32),
            pltpu.VMEM((4, 4, 4, 2, 8, 128), F32),
            pltpu.VMEM((4, 4, 3, 2, 8, 128), F32),
            pltpu.VMEM((4, 8, 8, 128), F32),
            pltpu.VMEM((8, 4, 8, 128), F32),
            pltpu.VMEM((16, 2, 8, 128), F32),
            dma((4,)),
            dma((4,)),
            dma((2, 4, 4)),
            dma((2, 4, 4)),
            dma((4, 4, 3)),
            dma((4, 4, 3)),
            dma((8, 4)),
            dma((8, 4)),
            dma((16,)),
            dma((16,)),
        ],
        compiler_params=pltpu.CompilerParams(
            collective_id=0, has_side_effects=True, vmem_limit_bytes=24 * 2**20
        ),
    )(
        wslot, tslot, wextra.reshape(4, 2, 4, 16, 2, 8, 128), textra,
        wide_table, wide_proj, thin_table, thin_proj.reshape(2, 128, 128),
    )


def local(wide_index, wide_table, wide_proj, thin_index, thin_table, thin_proj):
    wslot, tslot, wextra, textra = find(wide_index, thin_index, wide_table, wide_proj, thin_table)
    out = pool(wslot, tslot, wextra, textra, wide_table, wide_proj, thin_table, thin_proj)
    return out[:, :512], out[:, 512:]


def solution(mesh):
    placed = (P(), P(None, GX_GY, None), P(), P(None, None, "gx"), P(None, None, "gy"), P())
    return jax.shard_map(
        local,
        mesh=mesh,
        in_specs=placed,
        out_specs=(P(GX_GY, None), P(GX_GY, None)),
        check_vma=False,
    )
```

time: 53.4 us -> 45.3 us (0.85)
  Pallas kernels: 49.8 us -> 40.7 us
  local copies, waits for them, and re-layouts: 2.7 us -> 3.69 us
    pallas_call x2 -> x3, Pallas kernels: 49.8 us -> 40.7 us  [the longest x1 38.4 us: pool(): pl.pallas_call(pool_kernel, in_specs=[vmem] * 8, out_specs=vmem, out_shap...]
    unnamed x0 -> x12, local copies, waits for them, and re-layouts: none -> 2.47 us
    slice x2, local copies, waits for them, and re-layouts: 2.7 us -> 1.22 us  [local(): return (out[:, :512], out[:, 512:])]
where the time goes in v3:
time: 45.3 us; the launch traced here: 45.1 us
  Pallas kernels  40.7 us (90%)
  local copies, waits for them, and re-layouts  3.69 us (8%)
  between operations  0.68 us (2%)
    pallas_call x1, Pallas kernels, pool(): pl.pallas_call(pool_kernel, in_specs=[vmem] * 8, out_specs=vmem, out_shap...  38.4 us
    unnamed x12, local copies, waits for them, and re-layouts  2.47 us
    pallas_call x1, Pallas kernels, find(): pl.pallas_call(functools.partial(find_kernel, rows_w, rows_t), in_specs=[...  1.79 us
    slice x2, local copies, waits for them, and re-layouts, local(): return (out[:, :512], out[:, 512:])  1.22 us

profile of v3, /device:TPU:8, one launch (start us, length us, event | category | flops | bytes accessed | tf_op | source)
XLA Modules:
  0.0 45.1 jit_solution(11176420779413701034)
XLA Ops:
  0.6 0.0 copy-start.2
  0.6 1.2 %copy-done.2 = s32[4,32,2048]{2,1,0:T(8,128)S(1)} copy-done((s32[4,32,2048]{2,1,0:T(8,128)S(1)}, s32[4,32,2048]{2,1,0:T(8,128)}, u32[]{:S(2)}) %copy-start.2) | copy-done | bytes 1048600
  1.9 0.0 copy-start.4
  1.9 0.9 %copy-done.4 = s32[8,32,128]{2,1,0:T(8,128)S(1)} copy-done((s32[8,32,128]{2,1,0:T(8,128)S(1)}, s32[8,32,128]{2,1,0:T(8,128)}, u32[]{:S(2)}) %copy-start.4) | copy-done | bytes 131096
  2.8 0.0 copy-start
  2.8 0.0 copy-start.1
  2.8 0.0 copy-start.3
  2.8 1.8 %shard_map.77 = (f32[4,4,2048]{2,1,0:T(4,128)S(1)}, s32[8,12,128]{2,1,0:T(8,128)S(1)}, s32[4,1,2048]{2,1,0:T(1,128)S(1)}, s32[8,1,128]{2,1,0:T(1,128)S(1)}, s32[2,8,128]{2,1,0:T(8,128)S(1)}) custom-call(s32[4,32,2048]{2,1,0:T(8,128)S(1)} %copy-done.2, s32[8,32,128]{2,1,0:T(8,128)S(1)} %copy-done.4), custom_call_target="tpu_custom_call" | custom-call | flops 4000000000 | bytes 1048576 | tf_op jit(solution)/shard_map/pallas_call | solution.py:197
  4.6 0.0 copy-start.5
  4.6 0.0 copy-done
  4.6 0.0 copy-done.1
  4.6 0.0 copy-done.3
  4.7 0.5 %shard_map.78 = (f32[4,256,8,128]{3,2,1,0:T(8,128)S(1)}, f32[8,32,128]{2,1,0:T(8,128)S(1)}) custom-call(s32[4,32,2048]{2,1,0:T(8,128)S(1)} %copy-done.2, s32[8,32,128]{2,1,0:T(8,128)S(1)} %copy-done.4, s32[4,1,2048]{2,1,0:T(1,128)S(1)} %get-tuple-element.11.wmore, s32[8,1,128]{2,1,0:T(1,128)S(1)} %get-tuple-element.12.tmore, ...), custom_call_target="tpu_custom_call" | custom-call | tf_op jit(solution)/shard_map/pallas_call | solution.py:211
  5.2 0.3 copy-done.5
  5.4 38.4 %shard_map.79 = f32[8,1536]{1,0:T(8,128)S(1)} custom-call(f32[4,4,2048]{2,1,0:T(4,128)S(1)} %get-tuple-element.9.wslot, s32[8,12,128]{2,1,0:T(8,128)S(1)} %get-tuple-element.10.tslot, f32[4,2,4,16,2,8,128]{6,5,4,3,2,1,0:T(8,128)S(1)} %bitcast.2, f32[8,32,128]{2,1,0:T(8,128)S(1)} %get-tuple-element.15.textra, bf16[4,512,256]{2,1,0:T(8,128)(2,1)S(1)} %copy-done.1, ...), custom_call_target="tpu_custom_call" | custom-call | tf_op jit(solution)/shard_map/pallas_call | solution.py:453
  43.9 0.6 %slice.6 = f32[8,512]{1,0:T(8,128)} slice(f32[8,1536]{1,0:T(8,128)S(1)} %shard_map.79), slice={[0:8], [0:512]} | slice | bytes 32768 | tf_op jit(solution)/shard_map/slice | solution.py:492
  44.5 0.6 %slice.7 = f32[8,1024]{1,0:T(8,128)} slice(f32[8,1536]{1,0:T(8,128)S(1)} %shard_map.79), slice={[0:8], [512:1536]} | slice | bytes 65536 | tf_op jit(solution)/shard_map/slice | solution.py:492
Async XLA Ops:
  0.6 1.2 %copy-start.2 = (s32[4,32,2048]{2,1,0:T(8,128)S(1)}, s32[4,32,2048]{2,1,0:T(8,128)}, u32[]{:S(2)}) copy-start(s32[4,32,2048]{2,1,0:T(8,128)} %wi.3) | copy-start | bytes 3145732
  1.9 0.9 %copy-start.4 = (s32[8,32,128]{2,1,0:T(8,128)S(1)}, s32[8,32,128]{2,1,0:T(8,128)}, u32[]{:S(2)}) copy-start(s32[8,32,128]{2,1,0:T(8,128)} %ti.3) | copy-start | bytes 393220
  2.8 1.8 %copy-start = (bf16[8,32,4096]{2,1,0:T(8,128)(2,1)S(1)}, bf16[8,32,4096]{2,1,0:T(8,128)(2,1)}, u32[]{:S(2)}) copy-start(bf16[8,32,4096]{2,1,0:T(8,128)(2,1)} %tt.3) | copy-start | bytes 6291460
  2.8 1.9 %copy-start.1 = (bf16[4,512,256]{2,1,0:T(8,128)(2,1)S(1)}, bf16[4,512,256]{2,1,0:T(8,128)(2,1)}, u32[]{:S(2)}) copy-start(bf16[4,512,256]{2,1,0:T(8,128)(2,1)} %wt.3) | copy-start | bytes 3145732
  2.8 1.9 %copy-start.3 = (bf16[4,256,128]{2,1,0:T(8,128)(2,1)S(1)}, bf16[4,256,128]{2,1,0:T(8,128)(2,1)}, u32[]{:S(2)}) copy-start(bf16[4,256,128]{2,1,0:T(8,128)(2,1)} %wp.3) | copy-start | bytes 786436
  4.6 0.9 %copy-start.5 = (bf16[8,32,128]{2,1,0:T(8,128)(2,1)S(1)}, bf16[8,32,128]{2,1,0:T(8,128)(2,1)}, u32[]{:S(2)}) copy-start(bf16[8,32,128]{2,1,0:T(8,128)(2,1)} %param.11) | copy-start | bytes 196612
